TPU v7x, 32 devices: a whole 2x2x4 slice. The times are simulated.
32 devices in a mesh: fsdp: 4 (over x, core), tm: 8 (over z, y).
Axes of the slice: x: 2, y: 2, z: 4, core: 2. Of those that a mesh axis runs over, the one named last changes fastest.
Arguments:
- tokens: bfloat16 [8, 8, 256, 1024], P('fsdp', 'tm'), may hold values from -6 to 6
- spatial_gain: float32 [1024], replicated, may hold values from 0.25 to 1.75
- spatial_qkv: bfloat16 [1024, 1536], P('fsdp'), may hold values from -16 to 16
- spatial_out: bfloat16 [512, 1024], P('fsdp'), may hold values from -0.25 to 0.25
- temporal_gain: float32 [1024], replicated, may hold values from 0.25 to 1.75
- temporal_qkv: bfloat16 [1024, 1536], P('fsdp'), may hold values from -16 to 16
- temporal_out: bfloat16 [512, 1024], P('fsdp'), may hold values from -0.25 to 0.25
Outputs:
- encoded: bfloat16 [8, 8, 256, 1024], P('fsdp', 'tm')
All inputs are finite; a program needn't handle non-finite values.
Results may differ from a plain program's by a relative error of at most 0.0061.
Values may be sent and summed in bfloat16 or wider, within the bound.
A program may use at most 64 MiB of HBM per device.

v0:
```python
import jax
import jax.numpy as jnp
from jax import lax
from jax.sharding import PartitionSpec as P

HEAD = 64
HEADS = 8
INNER = 512
EPSILON = 1e-06


def norm_rows(source, norm_gain):
    values = source.astype(jnp.float32)
    centre = values - jnp.mean(values, axis=-1, keepdims=True)
    spread = jnp.mean(centre * centre, axis=-1, keepdims=True)
    return (centre * lax.rsqrt(spread + EPSILON) * norm_gain).astype(jnp.bfloat16)


def attention_core(projected):
    inner_width = projected.shape[-1] // 3
    lead_shape = projected.shape[:-1]
    queries = projected[..., :inner_width].reshape(lead_shape + (HEADS, HEAD))
    key_rows = projected[..., inner_width : 2 * inner_width].reshape(lead_shape + (HEADS, HEAD))
    value_rows = (
        projected[..., 2 * inner_width :].astype(jnp.bfloat16).reshape(lead_shape + (HEADS, HEAD))
    )
    scores = jnp.einsum(
        "blmhe,bkmhe->bmhlk", queries, key_rows, precision=lax.Precision.HIGHEST
    ) * HEAD ** (-0.5)
    row_max = jnp.max(scores, axis=-1, keepdims=True)
    exponent = jnp.exp(scores - row_max)
    weights = (exponent / jnp.sum(exponent, axis=-1, keepdims=True)).astype(jnp.bfloat16)
    context = jnp.einsum(
        "bmhlk,bkmhe->blmhe", weights, value_rows, preferred_element_type=jnp.float32
    )
    return context.astype(jnp.bfloat16).reshape(lead_shape + (inner_width,))


def project_inputs(normed, weight):

    def add_rows(running, segment, offset):
        return jnp.dot(normed, segment, preferred_element_type=jnp.float32)

    initial = jnp.zeros((normed.shape[0], weight.shape[1]), jnp.float32)
    return add_rows(initial, lax.all_gather(weight, "fsdp", axis=0, tiled=True), jnp.int32(0))


def project_outputs(context, weight):

    def add_rows(running, segment, offset):
        return jnp.dot(context, segment, preferred_element_type=jnp.float32)

    initial = jnp.zeros((context.shape[0], weight.shape[1]), jnp.float32)
    return add_rows(initial, lax.all_gather(weight, "fsdp", axis=0, tiled=True), jnp.int32(0))


def shards(
    tokens, spatial_gain, spatial_qkv, spatial_out, temporal_gain, temporal_qkv, temporal_out
):
    clip_count, frames, places, feature_width = tokens.shape
    row_count = clip_count * frames * places
    normed = norm_rows(tokens, spatial_gain).reshape(row_count, feature_width)
    projected = project_inputs(normed, spatial_qkv).reshape(
        clip_count * frames, places, 1, 3 * INNER
    )
    context = attention_core(projected).reshape(row_count, INNER)
    middle = (
        tokens.reshape(row_count, feature_width).astype(jnp.float32)
        + project_outputs(context, spatial_out)
    ).astype(jnp.bfloat16)
    middle = middle.reshape(clip_count, frames, places, feature_width)
    arrived = lax.all_to_all(middle, "tm", split_axis=2, concat_axis=1, tiled=True)
    full_frames = arrived.shape[1]
    few_places = arrived.shape[2]
    normed_t = norm_rows(arrived, temporal_gain).reshape(row_count, feature_width)
    projected_t = project_inputs(normed_t, temporal_qkv).reshape(
        clip_count, full_frames, few_places, 3 * INNER
    )
    context_t = attention_core(projected_t)
    returned_ctx = lax.all_to_all(context_t, "tm", split_axis=1, concat_axis=2, tiled=True)
    finished = middle.reshape(row_count, feature_width).astype(jnp.float32) + project_outputs(
        returned_ctx.reshape(row_count, INNER), temporal_out
    )
    return finished.astype(jnp.bfloat16).reshape(clip_count, frames, places, feature_width)


def solution(mesh):
    placed = (
        P("fsdp", "tm", None, None),
        P(),
        P("fsdp", None),
        P("fsdp", None),
        P(),
        P("fsdp", None),
        P("fsdp", None),
    )
    return jax.shard_map(
        shards, mesh=mesh, in_specs=placed, out_specs=P("fsdp", "tm", None, None), check_vma=False
    )
```

profile of v0, /device:TPU:0, one launch (start us, length us, event | category | flops | bytes accessed | tf_op | source)
XLA Modules:
  0.0 167.2 jit_solution(3869164747820133010)
XLA Ops:
  9.4 30.8 %all-gather.5.cloned.1.call-done = bf16[1024,1536]{1,0:T(8,128)(2,1)} async-done(((bf16[256,1536]{1,0:T(8,128)(2,1)}), bf16[1024,1536]{1,0:T(8,128)(2,1)}) %all-gather.5.cloned.1.call-update) | async-done | bytes 3145744 | tf_op jit(solution)/shard_map/all_gather | solution.py:45
  40.2 3.8 %convolution_bitcast_fusion = f32[2,256,1,1536]{3,1,0,2:T(8,128)S(1)} fusion(bf16[1024,1536]{1,0:T(8,128)(2,1)} %all-gather.5.cloned.1.call-done, bf16[2,1,256,1024]{3,2,1,0:T(8,128)(2,1)S(1)} %copy-done, f32[1024]{0:T(1024)S(1)} %copy-done.5, f32[2,256]{1,0:T(2,128)S(1)} %add_rsqrt_fusion.1, f32[2,256]{1,0:T(2,128)S(1)} %broadcast_multiply_fusion.1), kind=kOutput, calls=%fused_computation.6 | convolution fusion | flops 1613234176 | bytes 7348224 | tf_op jit(solution)/shard_map/dot_general | solution.py:42
  44.0 1.7 %copy-done.1 = f32[2,256,1,1536]{3,1,0,2:T(8,128)} copy-done((f32[2,256,1,1536]{3,1,0,2:T(8,128)}, f32[2,256,1,1536]{3,1,0,2:T(8,128)S(1)}, u32[]{:S(2)}) %copy-start.1) | copy-done | bytes 3145752
  45.7 1.0 copy.81
  46.7 2.8 %fusion.36 = (f32[2,256,1,512]{3,1,0,2:T(8,128)S(1)}, f32[2,256,1,512]{3,1,0,2:T(8,128)}) fusion(f32[2,256,1,1536]{3,1,0,2:T(8,128)} %copy-done.1), kind=kLoop, calls=%fused_computation.54 | loop fusion | bytes 4194304 | tf_op jit(solution)/shard_map/slice | solution.py:23
  49.5 1.6 copy.82
  51.1 1.3 copy.83
  52.4 4.7 %fusion.39 = f32[2,8,256,256]{2,3,1,0:T(8,128)S(1)} fusion(f32[2,256,8,64]{1,3,2,0:T(8,128)S(1)} %bitcast.58, f32[2,256,8,64]{1,3,2,0:T(8,128)} %bitcast.59), kind=kOutput, calls=%fused_computation.57 | convolution fusion | flops 805306368 | bytes 6291456 | tf_op jit(solution)/shard_map/blmhe,bkmhe->bmhlk/dot_general | solution.py:27
  57.2 3.2 %fusion.37 = (f32[2,8,256]{2,1,0:T(8,128)S(1)}, f32[2,8,256,256]{2,3,1,0:T(8,128)S(1)}) fusion(f32[2,8,256,256]{2,3,1,0:T(8,128)S(1)} %fusion.39), kind=kOutput, calls=%fused_computation.55 | output fusion | flops 4194559 | bytes 8404992 | tf_op jit(solution)/shard_map/sub | solution.py:31
  61.6 2.0 %fusion.8 = bf16[512,1024]{1,0:T(8,128)(2,1)S(1)} fusion(bf16[2,1,256,1024]{3,2,1,0:T(8,128)(2,1)S(1)} %copy-done, bf16[512,512]{0,1:T(8,128)(2,1)S(1)} %bitcast.65, bf16[512,1024]{1,0:T(8,128)(2,1)} %all-gather.7.cloned.1.call-done), kind=kOutput, calls=%fused_computation.11 | convolution fusion | flops 538443776 | bytes 3670016 | tf_op jit(solution)/shard_map/dot_general | solution.py:51
  64.5 2.0 %copy.86 = bf16[2,1,256,1024]{3,0,1,2:T(2,128)(2,1)} copy(bf16[2,1,256,1024]{3,2,0,1:T(8,128)(2,1)S(1)} %bitcast.62) | data formatting | bytes 2097152 | tf_op jit(solution)/shard_map/reshape | solution.py:71
  66.6 5.5 %all-to-all-start = ((bf16[2,1,256,1024]{3,0,1,2:T(2,128)(2,1)}), bf16[2,1,256,1024]{3,0,1,2:T(2,128)(2,1)S(1)}, u32[]{:S(2)}, u32[]{:S(2)}) async-start(bf16[2,1,256,1024]{3,0,1,2:T(2,128)(2,1)} %copy.86), calls=%async_computation | async-start | bytes 2097152 | tf_op jit(solution)/shard_map/all_to_all | solution.py:72
  72.6 25.6 %all-to-all-done = bf16[2,1,256,1024]{3,0,1,2:T(2,128)(2,1)S(1)} async-done(((bf16[2,1,256,1024]{3,0,1,2:T(2,128)(2,1)}), bf16[2,1,256,1024]{3,0,1,2:T(2,128)(2,1)S(1)}, u32[]{:S(2)}, u32[]{:S(2)}) %all-to-all-start) | async-done | bytes 1048608 | tf_op jit(solution)/shard_map/all_to_all | solution.py:72
  99.9 2.0 %multiply_reduce_fusion.1 = f32[2,256]{0,1:T(8,128)S(1)} fusion(bf16[2,1,256,1024]{3,0,1,2:T(2,128)(2,1)S(1)} %all-to-all-done, f32[2,256]{0,1:T(8,128)S(1)} %broadcast_multiply_fusion), kind=kLoop, calls=%fused_computation.22 | loop fusion | flops 2096640 | bytes 1052672 | tf_op jit(solution)/shard_map/reduce_sum | solution.py:15
  102.2 4.0 %fusion.5 = f32[2,8,32,1536]{3,2,1,0:T(8,128)S(1)} fusion(bf16[1024,1536]{1,0:T(8,128)(2,1)} %all-gather.9.cloned.1.call-done, f32[2,8,32,1024]{3,0,2,1:T(2,128)S(1)} %convert.12, f32[1024]{0:T(1024)S(1)} %copy-done.6, f32[2,8,32]{2,1,0:T(8,128)S(1)} %copy.121, f32[2,8,32]{2,1,0:T(8,128)S(1)} %copy.122), kind=kOutput, calls=%fused_computation.7 | convolution fusion | flops 1612709888 | bytes 8396800 | tf_op jit(solution)/shard_map/dot_general | solution.py:42
  106.2 1.1 fusion.35
  108.2 1.6 reshape.157
  109.8 1.8 %reshape.156 = f32[2,8,32,8,64]{4,3,2,1,0:T(8,128)} reshape(f32[2,8,32,512]{3,2,1,0:T(8,128)S(1)} %get-tuple-element.5) | data formatting | bytes 2097152 | tf_op jit(solution)/shard_map/reshape | solution.py:22
  111.6 1.6 reshape.155
  113.2 7.9 %fusion.9 = f32[2,32,8,8,8]{3,4,2,1,0:T(8,128)S(1)} fusion(f32[2,8,32,8,64]{4,3,2,1,0:T(8,128)S(1)} %reshape.157, f32[2,8,32,8,64]{4,3,2,1,0:T(8,128)} %reshape.156), kind=kOutput, calls=%fused_computation.12 | convolution fusion | flops 25165824 | bytes 2228224 | tf_op jit(solution)/shard_map/blmhe,bkmhe->bmhlk/dot_general | solution.py:27
  121.1 16.6 %fusion.38 = (f32[2,32,8,8]{3,2,1,0:T(8,128)S(1)}, f32[2,32,8,8,8]{3,4,2,1,0:T(8,128)S(1)}) fusion(f32[2,32,8,8,8]{3,4,2,1,0:T(8,128)S(1)} %fusion.9), kind=kOutput, calls=%fused_computation.56 | output fusion | flops 98311 | bytes 278528 | tf_op jit(solution)/shard_map/sub | solution.py:31
  137.7 1.0 fusion.18
  139.6 18.1 %all_to_all.8 = bf16[2,8,32,512]{3,2,0,1:T(8,128)(2,1)S(1)} all-to-all(bf16[2,8,32,512]{3,2,0,1:T(8,128)(2,1)S(1)} %reshape.165), channel_id=1, replica_groups=mesh['fsdp'=4,'tm'=8] {'tm'}, dimensions={1} | all-to-all | bytes 1048576 | tf_op jit(solution)/shard_map/all_to_all | solution.py:80
  157.7 2.9 %add_convert_fusion = bf16[512,1024]{1,0:T(8,128)(2,1)} fusion(bf16[512,1024]{1,0:T(8,128)(2,1)S(1)} %copy-done.3, bf16[512,512]{1,0:T(8,128)(2,1)S(1)} %bitcast.64, bf16[512,1024]{1,0:T(8,128)(2,1)} %all-gather.11.cloned.1.call-done), kind=kOutput, calls=%fused_computation.19 | convolution fusion | flops 538443776 | bytes 3670016 | tf_op jit(solution)/shard_map/dot_general | solution.py:51
  (42 shorter events, 9.2 us)
Async XLA Ops:
  6.5 2.2 %copy-start = (bf16[2,1,256,1024]{3,2,1,0:T(8,128)(2,1)S(1)}, bf16[2,1,256,1024]{3,2,1,0:T(8,128)(2,1)}, u32[]{:S(2)}) copy-start(bf16[2,1,256,1024]{3,2,1,0:T(8,128)(2,1)} %param.7) | copy-start | bytes 3145732
  6.5 33.6 %copy-start.5 = (f32[1024]{0:T(1024)S(1)}, f32[1024]{0:T(1024)}, u32[]{:S(2)}) copy-start(f32[1024]{0:T(1024)} %param.8) | copy-start | bytes 12292
  6.5 33.6 %all-gather.5.cloned.1.call-start = ((), (), s32[]{:S(2)}) async-start(), calls=%async_computation.2 | async-start | bytes 3932160 | tf_op jit(solution)/shard_map/all_gather | solution.py:45
  7.3 54.3 %all-gather.7.cloned.1.call-start = ((), (), s32[]{:S(2)}) async-start(), calls=%async_computation.3 | async-start | bytes 1310720 | tf_op jit(solution)/shard_map/all_gather | solution.py:54
  8.0 94.2 %all-gather.9.cloned.1.call-start = ((), (), s32[]{:S(2)}) async-start(), calls=%async_computation.4 | async-start | bytes 3932160 | tf_op jit(solution)/shard_map/all_gather | solution.py:45
  44.0 1.7 %copy-start.1 = (f32[2,256,1,1536]{3,1,0,2:T(8,128)}, f32[2,256,1,1536]{3,1,0,2:T(8,128)S(1)}, u32[]{:S(2)}) copy-start(f32[2,256,1,1536]{3,1,0,2:T(8,128)S(1)} %convolution_bitcast_fusion) | copy-start | bytes 9437188
  57.2 3.3 %copy-start.4 = (bf16[2,256,1,512]{1,3,0,2:T(8,128)(2,1)S(1)}, bf16[2,256,1,512]{1,3,0,2:T(8,128)(2,1)}, u32[]{:S(2)}) copy-start(bf16[2,256,1,512]{1,3,0,2:T(8,128)(2,1)} %copy.81) | copy-start | bytes 1572868
  63.6 1.0 copy-start.2
  66.6 31.7 %all-to-all-start = ((bf16[2,1,256,1024]{3,0,1,2:T(2,128)(2,1)}), bf16[2,1,256,1024]{3,0,1,2:T(2,128)(2,1)S(1)}, u32[]{:S(2)}, u32[]{:S(2)}) async-start(bf16[2,1,256,1024]{3,0,1,2:T(2,128)(2,1)} %copy.86), calls=%async_computation | async-start | bytes 2097152 | tf_op jit(solution)/shard_map/all_to_all | solution.py:72
  72.1 85.6 %all-gather.11.cloned.1.call-start = ((), (), s32[]{:S(2)}) async-start(), calls=%async_computation.5 | async-start | bytes 1310720 | tf_op jit(solution)/shard_map/all_gather | solution.py:54
  99.0 3.2 %copy-start.6 = (f32[1024]{0:T(1024)S(1)}, f32[1024]{0:T(1024)}, u32[]{:S(2)}) copy-start(f32[1024]{0:T(1024)} %param.11) | copy-start | bytes 12292
  138.9 18.8 %copy-start.3 = (bf16[512,1024]{1,0:T(8,128)(2,1)S(1)}, bf16[512,1024]{1,0:T(8,128)(2,1)}, u32[]{:S(2)}) copy-start(bf16[512,1024]{1,0:T(8,128)(2,1)} %copy-done.2) | copy-start | bytes 3145732
Sparse Core Ops, SparseCore 0:
  8.9 31.2 all-gather.4
  41.7 16.6 all-gather.6
  60.0 28.4 all-gather.8
  90.0 16.6 all-gather.10
where the time goes:
time: 168 us; the launch traced here: 167 us
  waiting for transfers between devices  59 us (35%)
  matrix products  26.8 us (16%)
  other arithmetic  24.1 us (14%)
  local copies, waits for them, and re-layouts  20.1 us (12%)
  blocking collectives  18.1 us (11%)
  between operations  13.4 us (8%)
  starting transfers between devices  5.61 us (3%)
    all_gather x2, waiting for transfers between devices, project_inputs(): lax.all_gather(weight, 'fsdp', axis=0, tiled=True)  30.8 us
    all_to_all x1, waiting for transfers between devices, shards(): lax.all_to_all(middle, 'tm', split_axis=2, concat_axis=1, tiled=True)  25.6 us
    sub x2, other arithmetic, attention_core(): exponent = jnp.exp(scores - row_max)  19.8 us
    all_to_all x1, blocking collectives, shards(): lax.all_to_all(context_t, 'tm', split_axis=1, concat_axis=2, tiled=True)  18.1 us
    dot_general x2, matrix products, attention_core(): jnp.einsum('blmhe,bkmhe->bmhlk', queries, key_rows, precision=lax.Precisi...  12.6 us
    dot_general x2, matrix products, add_rows(): return jnp.dot(normed, segment, preferred_element_type=jnp.float32)  7.81 us
    all_to_all x1, starting transfers between devices, shards(): lax.all_to_all(middle, 'tm', split_axis=2, concat_axis=1, tiled=True)  5.5 us
    dot_general x2, matrix products, add_rows(): return jnp.dot(context, segment, preferred_element_type=jnp.float32)  4.86 us
  transfers between devices with their start and end apart: 5, of which 2 were waited for; matrix products, arithmetic and copies ran while one was open for 39% of the time, Pallas kernels for 0%

commit v1 on v0

--- a/solution.py
+++ b/solution.py
@@ -77,7 +77,10 @@
         clip_count, full_frames, few_places, 3 * INNER
     )
     context_t = attention_core(projected_t)
-    returned_ctx = lax.all_to_all(context_t, "tm", split_axis=1, concat_axis=2, tiled=True)
+    returned_ctx = jnp.concatenate(
+        lax.all_to_all(jnp.stack(jnp.split(context_t, lax.axis_size("tm"), axis=1)), "tm", 0, 0),
+        axis=2,
+    )
     finished = middle.reshape(row_count, feature_width).astype(jnp.float32) + project_outputs(
         returned_ctx.reshape(row_count, INNER), temporal_out
     )

time: 168 us -> 154 us (0.917)
  other arithmetic: 24.1 us -> 9.64 us
    sub x2, other arithmetic: 19.8 us -> 5.53 us  [attention_core(): exponent = jnp.exp(scores - row_max)]
  transfers between devices with their start and end apart: 5 -> 5, of which waited for: 2 -> 2; matrix products, arithmetic and copies ran while one was open for 39% -> 34% of each run, Pallas kernels for 0% -> 0%
where the time goes in v1:
time: 154 us; the launch traced here: 153 us
  waiting for transfers between devices  58.8 us (38%)
  matrix products  28.3 us (18%)
  local copies, waits for them, and re-layouts  19.1 us (12%)
  blocking collectives  18.1 us (12%)
  between operations  13.4 us (9%)
  other arithmetic  9.64 us (6%)
  starting transfers between devices  5.79 us (4%)
    all_gather x2, waiting for transfers between devices, project_inputs(): lax.all_gather(weight, 'fsdp', axis=0, tiled=True)  30.8 us
    all_to_all x1, waiting for transfers between devices, shards(): lax.all_to_all(middle, 'tm', split_axis=2, concat_axis=1, tiled=True)  25.6 us
    all_to_all x1, blocking collectives, shards(): lax.all_to_all(jnp.stack(jnp.split(context_t, lax.axis_size('tm'), axis=1...  18.1 us
    dot_general x2, matrix products, attention_core(): jnp.einsum('blmhe,bkmhe->bmhlk', queries, key_rows, precision=lax.Precisi...  12.6 us
    dot_general x2, matrix products, add_rows(): return jnp.dot(normed, segment, preferred_element_type=jnp.float32)  7.8 us
    sub x2, other arithmetic, attention_core(): exponent = jnp.exp(scores - row_max)  5.53 us
    all_to_all x1, starting transfers between devices, shards(): lax.all_to_all(middle, 'tm', split_axis=2, concat_axis=1, tiled=True)  5.49 us
    dot_general x2, matrix products, add_rows(): return jnp.dot(context, segment, preferred_element_type=jnp.float32)  4.86 us
  transfers between devices with their start and end apart: 5, of which 2 were waited for; matrix products, arithmetic and copies ran while one was open for 34% of the time, Pallas kernels for 0%

profile of v1, /device:TPU:0, one launch (start us, length us, event | category | flops | bytes accessed | tf_op | source)
XLA Modules:
  0.0 153.2 jit_solution(6390045680826206325)
XLA Ops:
  9.4 30.8 %all-gather.5.cloned.1.call-done = bf16[1024,1536]{1,0:T(8,128)(2,1)} async-done(((bf16[256,1536]{1,0:T(8,128)(2,1)}), bf16[1024,1536]{1,0:T(8,128)(2,1)}) %all-gather.5.cloned.1.call-update) | async-done | bytes 3145744 | tf_op jit(solution)/shard_map/all_gather | solution.py:45
  40.2 3.8 %convolution_bitcast_fusion = f32[2,256,1,1536]{3,1,0,2:T(8,128)S(1)} fusion(bf16[1024,1536]{1,0:T(8,128)(2,1)} %all-gather.5.cloned.1.call-done, bf16[2,1,256,1024]{3,2,1,0:T(8,128)(2,1)S(1)} %copy-done, f32[1024]{0:T(1024)S(1)} %copy-done.6, f32[2,256]{1,0:T(2,128)S(1)} %add_rsqrt_fusion.1, f32[2,256]{1,0:T(2,128)S(1)} %broadcast_multiply_fusion.1), kind=kOutput, calls=%fused_computation.6 | convolution fusion | flops 1613234176 | bytes 7348224 | tf_op jit(solution)/shard_map/dot_general | solution.py:42
  44.0 1.7 %copy-done.1 = f32[2,256,1,1536]{3,1,0,2:T(8,128)} copy-done((f32[2,256,1,1536]{3,1,0,2:T(8,128)}, f32[2,256,1,1536]{3,1,0,2:T(8,128)S(1)}, u32[]{:S(2)}) %copy-start.1) | copy-done | bytes 3145752
  45.7 1.0 copy.90
  46.7 2.8 %fusion.44 = (f32[2,256,1,512]{3,1,0,2:T(8,128)S(1)}, f32[2,256,1,512]{3,1,0,2:T(8,128)}) fusion(f32[2,256,1,1536]{3,1,0,2:T(8,128)} %copy-done.1), kind=kLoop, calls=%fused_computation.70 | loop fusion | bytes 4194304 | tf_op jit(solution)/shard_map/slice | solution.py:23
  49.5 1.6 %copy.91 = f32[2,256,1,512]{1,3,0,2:T(8,128)S(1)} copy(f32[2,256,1,512]{3,1,0,2:T(8,128)} %get-tuple-element.8) | data formatting | bytes 2097152 | tf_op jit(solution)/shard_map/slice | solution.py:22
  51.1 1.3 copy.92
  52.4 4.8 %fusion.47 = f32[2,8,256,256]{2,3,1,0:T(8,128)S(1)} fusion(f32[2,256,8,64]{1,3,2,0:T(8,128)S(1)} %bitcast.103, f32[2,256,8,64]{1,3,2,0:T(8,128)} %bitcast.104), kind=kOutput, calls=%fused_computation.73 | convolution fusion | flops 805306368 | bytes 6291456 | tf_op jit(solution)/shard_map/blmhe,bkmhe->bmhlk/dot_general | solution.py:27
  57.2 3.2 %fusion.45 = (f32[2,8,256]{2,1,0:T(8,128)S(1)}, f32[2,8,256,256]{2,3,1,0:T(8,128)S(1)}) fusion(f32[2,8,256,256]{2,3,1,0:T(8,128)S(1)} %fusion.47), kind=kOutput, calls=%fused_computation.71 | output fusion | flops 4194559 | bytes 8404992 | tf_op jit(solution)/shard_map/sub | solution.py:31
  61.6 2.0 %fusion.8 = bf16[512,1024]{1,0:T(8,128)(2,1)S(1)} fusion(bf16[2,1,256,1024]{3,2,1,0:T(8,128)(2,1)S(1)} %copy-done, bf16[512,512]{0,1:T(8,128)(2,1)S(1)} %bitcast.111, bf16[512,1024]{1,0:T(8,128)(2,1)} %all-gather.7.cloned.1.call-done), kind=kOutput, calls=%fused_computation.11 | convolution fusion | flops 538443776 | bytes 3670016 | tf_op jit(solution)/shard_map/dot_general | solution.py:51
  63.6 1.0 copy-done.3
  64.5 2.1 %copy.95 = bf16[2,1,256,1024]{3,0,1,2:T(2,128)(2,1)} copy(bf16[2,1,256,1024]{3,2,0,1:T(8,128)(2,1)S(1)} %bitcast.108) | data formatting | bytes 2097152 | tf_op jit(solution)/shard_map/reshape | solution.py:71
  66.6 5.5 %all-to-all-start = ((bf16[2,1,256,1024]{3,0,1,2:T(2,128)(2,1)}), bf16[2,1,256,1024]{3,0,1,2:T(2,128)(2,1)S(1)}, u32[]{:S(2)}, u32[]{:S(2)}) async-start(bf16[2,1,256,1024]{3,0,1,2:T(2,128)(2,1)} %copy.95), calls=%async_computation | async-start | bytes 2097152 | tf_op jit(solution)/shard_map/all_to_all | solution.py:72
  72.7 25.6 %all-to-all-done = bf16[2,1,256,1024]{3,0,1,2:T(2,128)(2,1)S(1)} async-done(((bf16[2,1,256,1024]{3,0,1,2:T(2,128)(2,1)}), bf16[2,1,256,1024]{3,0,1,2:T(2,128)(2,1)S(1)}, u32[]{:S(2)}, u32[]{:S(2)}) %all-to-all-start) | async-done | bytes 1048608 | tf_op jit(solution)/shard_map/all_to_all | solution.py:72
  99.9 1.8 %multiply_reduce_fusion.1 = f32[2,256]{0,1:T(8,128)S(1)} fusion(bf16[2,1,256,1024]{3,0,1,2:T(2,128)(2,1)S(1)} %all-to-all-done, f32[2,256]{0,1:T(8,128)S(1)} %broadcast_multiply_fusion), kind=kLoop, calls=%fused_computation.22 | loop fusion | flops 2096640 | bytes 1052672 | tf_op jit(solution)/shard_map/reduce_sum | solution.py:15
  102.0 4.0 %fusion.5 = f32[2,8,32,1536]{3,2,1,0:T(8,128)S(1)} fusion(bf16[1024,1536]{1,0:T(8,128)(2,1)} %all-gather.9.cloned.1.call-done, f32[2,8,32,1024]{3,0,2,1:T(2,128)S(1)} %convert.12, f32[1024]{0:T(1024)S(1)} %copy-done.7, f32[2,8,32]{2,1,0:T(8,128)S(1)} %copy.141, f32[2,8,32]{2,1,0:T(8,128)S(1)} %copy.142), kind=kOutput, calls=%fused_computation.7 | convolution fusion | flops 1612709888 | bytes 8396800 | tf_op jit(solution)/shard_map/dot_general | solution.py:42
  106.0 1.1 fusion.43
  108.0 1.6 %reshape.153 = f32[2,8,32,8,64]{4,3,2,1,0:T(8,128)S(1)} reshape(f32[2,8,32,512]{3,2,1,0:T(8,128)} %get-tuple-element.6) | data formatting | bytes 2097152 | tf_op jit(solution)/shard_map/reshape | solution.py:23
  109.6 1.8 %reshape.152 = f32[2,8,32,8,64]{4,3,2,1,0:T(8,128)} reshape(f32[2,8,32,512]{3,2,1,0:T(8,128)S(1)} %get-tuple-element.5) | data formatting | bytes 2097152 | tf_op jit(solution)/shard_map/reshape | solution.py:22
  111.4 7.9 %fusion.9 = f32[2,32,8,8,8]{3,4,2,1,0:T(8,128)S(1)} fusion(f32[2,8,32,8,64]{4,3,2,1,0:T(8,128)S(1)} %reshape.153, f32[2,8,32,8,64]{4,3,2,1,0:T(8,128)} %reshape.152), kind=kOutput, calls=%fused_computation.12 | convolution fusion | flops 25165824 | bytes 2228224 | tf_op jit(solution)/shard_map/blmhe,bkmhe->bmhlk/dot_general | solution.py:27
  119.3 2.3 %fusion.46 = (f32[2,32,8,8]{3,2,1,0:T(8,128)S(1)}, f32[2,32,8,8,8]{3,4,2,1,0:T(8,128)}) fusion(f32[2,32,8,8,8]{3,4,2,1,0:T(8,128)S(1)} %fusion.9), kind=kOutput, calls=%fused_computation.72 | output fusion | flops 98311 | bytes 278528 | tf_op jit(solution)/shard_map/sub | solution.py:31
  122.1 2.6 %fusion.18 = bf16[2,8,32,8,64]{4,1,3,2,0:T(8,128)(2,1)S(1)} fusion(f32[2,32,8,8,8]{3,4,2,1,0:T(8,128)} %get-tuple-element.12, bf16[2,8,32,8,64]{4,3,2,1,0:T(8,128)(2,1)S(1)} %reshape.151, f32[2,32,8,8]{3,2,1,0:T(8,128)S(1)} %get-tuple-element.11), kind=kOutput, calls=%fused_computation.31 | convolution fusion | flops 4521984 | bytes 1196032 | tf_op jit(solution)/shard_map/bmhlk,bkmhe->blmhe/dot_general | solution.py:33
  125.6 18.1 %all_to_all.14 = bf16[8,2,1,32,512]{4,3,1,2,0:T(8,128)(2,1)S(1)} all-to-all(bf16[8,2,1,32,512]{4,3,1,2,0:T(8,128)(2,1)S(1)} %fusion.33), channel_id=1, replica_groups=mesh['fsdp'=4,'tm'=8] {'tm'}, dimensions={0} | all-to-all | bytes 1048576 | tf_op jit(solution)/shard_map/all_to_all | solution.py:81
  143.8 2.9 %add_convert_fusion = bf16[512,1024]{1,0:T(8,128)(2,1)} fusion(bf16[512,1024]{1,0:T(8,128)(2,1)S(1)} %copy-done.4, bf16[512,512]{1,0:T(8,128)(2,1)S(1)} %bitcast.110, bf16[512,1024]{1,0:T(8,128)(2,1)} %all-gather.11.cloned.1.call-done), kind=kOutput, calls=%fused_computation.19 | convolution fusion | flops 538443776 | bytes 3670016 | tf_op jit(solution)/shard_map/dot_general | solution.py:51
  (52 shorter events, 8.8 us)
Async XLA Ops:
  6.5 2.2 %copy-start = (bf16[2,1,256,1024]{3,2,1,0:T(8,128)(2,1)S(1)}, bf16[2,1,256,1024]{3,2,1,0:T(8,128)(2,1)}, u32[]{:S(2)}) copy-start(bf16[2,1,256,1024]{3,2,1,0:T(8,128)(2,1)} %param.7) | copy-start | bytes 3145732
  6.5 33.6 %copy-start.6 = (f32[1024]{0:T(1024)S(1)}, f32[1024]{0:T(1024)}, u32[]{:S(2)}) copy-start(f32[1024]{0:T(1024)} %param.8) | copy-start | bytes 12292
  6.5 33.6 %all-gather.5.cloned.1.call-start = ((), (), s32[]{:S(2)}) async-start(), calls=%async_computation.2 | async-start | bytes 3932160 | tf_op jit(solution)/shard_map/all_gather | solution.py:45
  7.3 54.3 %all-gather.7.cloned.1.call-start = ((), (), s32[]{:S(2)}) async-start(), calls=%async_computation.3 | async-start | bytes 1310720 | tf_op jit(solution)/shard_map/all_gather | solution.py:54
  8.0 94.0 %all-gather.9.cloned.1.call-start = ((), (), s32[]{:S(2)}) async-start(), calls=%async_computation.4 | async-start | bytes 3932160 | tf_op jit(solution)/shard_map/all_gather | solution.py:45
  44.0 1.7 %copy-start.1 = (f32[2,256,1,1536]{3,1,0,2:T(8,128)}, f32[2,256,1,1536]{3,1,0,2:T(8,128)S(1)}, u32[]{:S(2)}) copy-start(f32[2,256,1,1536]{3,1,0,2:T(8,128)S(1)} %convolution_bitcast_fusion) | copy-start | bytes 9437188
  57.2 3.3 %copy-start.5 = (bf16[2,256,1,512]{1,3,0,2:T(8,128)(2,1)S(1)}, bf16[2,256,1,512]{1,3,0,2:T(8,128)(2,1)}, u32[]{:S(2)}) copy-start(bf16[2,256,1,512]{1,3,0,2:T(8,128)(2,1)} %copy.90) | copy-start | bytes 1572868
  63.6 1.0 copy-start.3
  66.6 31.7 %all-to-all-start = ((bf16[2,1,256,1024]{3,0,1,2:T(2,128)(2,1)}), bf16[2,1,256,1024]{3,0,1,2:T(2,128)(2,1)S(1)}, u32[]{:S(2)}, u32[]{:S(2)}) async-start(bf16[2,1,256,1024]{3,0,1,2:T(2,128)(2,1)} %copy.95), calls=%async_computation | async-start | bytes 2097152 | tf_op jit(solution)/shard_map/all_to_all | solution.py:72
  72.1 71.7 %all-gather.11.cloned.1.call-start = ((), (), s32[]{:S(2)}) async-start(), calls=%async_computation.5 | async-start | bytes 1310720 | tf_op jit(solution)/shard_map/all_gather | solution.py:54
  99.0 3.0 %copy-start.7 = (f32[1024]{0:T(1024)S(1)}, f32[1024]{0:T(1024)}, u32[]{:S(2)}) copy-start(f32[1024]{0:T(1024)} %param.11) | copy-start | bytes 12292
  119.3 2.3 %copy-start.2 = (bf16[2,8,32,512]{3,2,1,0:T(8,128)(2,1)S(1)}, bf16[2,8,32,512]{3,2,1,0:T(8,128)(2,1)}, u32[]{:S(2)}) copy-start(bf16[2,8,32,512]{3,2,1,0:T(8,128)(2,1)} %slice.34) | copy-start | bytes 1572868
  124.9 18.9 %copy-start.4 = (bf16[512,1024]{1,0:T(8,128)(2,1)S(1)}, bf16[512,1024]{1,0:T(8,128)(2,1)}, u32[]{:S(2)}) copy-start(bf16[512,1024]{1,0:T(8,128)(2,1)} %copy-done.3) | copy-start | bytes 3145732
Sparse Core Ops, SparseCore 0:
  8.9 31.2 all-gather.4
  41.7 16.6 all-gather.6
  60.0 28.4 all-gather.8
  90.0 16.6 all-gather.10
